TPU v7x, 256 devices: a whole 4x4x8 slice. The times are simulated.
256 devices in a mesh: cluster: 64 (over x, z, core), dir: 4 (over y).
Axes of the slice: x: 4, y: 4, z: 8, core: 2. Of those that a mesh axis runs over, the one named last changes fastest.
Arguments:
- ray_code: int32 [1024, 524288], P('dir', 'cluster'), may hold values from 0 to 16, as said below
- occluder_list: int32 [64, 16], replicated, may hold values from 0 to 511, as said below
- list_count: int32 [64], replicated, may hold values from 1 to 16, 768 in all
- normal_azimuth: float32 [524288], P('cluster'), may hold values from -3.140625 to 3.140625
- normal_height: float32 [524288], P('cluster'), may hold values from -1 to 1
- albedo: float32 [524288], P('cluster'), may hold values from 0.2 to 1
- occluder_exit_radiance: bfloat16 [512, 81, 1024], P('cluster', None, 'dir'), may hold values from -18 to 18
Outputs:
- transfer: bfloat16 [81, 524288], P(None, ('cluster', 'dir'))
Inputs may be any that keep to these rules, and one draw needn't show every extreme that they name: `occluder_list`: each row names 16 different blocks, exactly 2 held by each of 8 different clusters; block b is held by cluster b // 8. `list_count`: entry c is the number of leading slots of row c of occluder_list in use. `ray_code`: A code of a vertex of cluster c below list_count[c] names the slot of that cluster's list whose block the ray ends on; any other code means the ray escapes.
All inputs are finite; a program needn't handle non-finite values.
Results may differ from a plain program's by a relative error of at most 0.0041.
Values may be sent and summed in bfloat16 or wider, within the bound.
A program may use at most 128 MiB of HBM per device.

v0:
```python
import math

import jax
import jax.numpy as jnp
from jax import lax
from jax.sharding import PartitionSpec as P

NDIR = 1024
SHORD = 9


golden_angle = math.pi * (3.0 - math.sqrt(5.0))


def sphere_points(direction_index, direction_overall_count):
    position = direction_index.astype(jnp.float32)
    along_z = 1.0 - (2.0 * position + 1.0) / direction_overall_count
    radius = jnp.sqrt(jnp.maximum(1.0 - along_z * along_z, 0.0))
    turned = position * golden_angle
    return (radius * jnp.cos(turned), radius * jnp.sin(turned), along_z)


def harmonic_table(along_x, along_y, along_z, degrees):
    cosine_terms = [jnp.ones_like(along_x)]
    sine_terms = [jnp.zeros_like(along_x)]
    for power_exponent in range(1, degrees):
        cosine_terms.append(cosine_terms[-1] * along_x - sine_terms[-1] * along_y)
        sine_terms.append(cosine_terms[-2] * along_y + sine_terms[-1] * along_x)
    basis_rows = [None] * (degrees * degrees)
    for order_index in range(degrees):
        diagonal_entries = 1.0
        for factor in range(1, 2 * order_index, 2):
            diagonal_entries = diagonal_entries * factor
        legendre = [None] * degrees
        legendre[order_index] = jnp.full_like(along_z, diagonal_entries)
        if order_index + 1 < degrees:
            legendre[order_index + 1] = along_z * ((2 * order_index + 1) * diagonal_entries)
        for degree in range(order_index + 2, degrees):
            legendre[degree] = (
                (2 * degree - 1) * along_z * legendre[degree - 1]
                - (degree + order_index - 1) * legendre[degree - 2]
            ) / (degree - order_index)
        for degree in range(order_index, degrees):
            factor_norm = math.sqrt(
                (2 * degree + 1)
                / (4.0 * math.pi)
                * math.factorial(degree - order_index)
                / math.factorial(degree + order_index)
            )
            centre = degree * degree + degree
            if order_index == 0:
                basis_rows[centre] = factor_norm * legendre[degree]
            else:
                basis_rows[centre + order_index] = (
                    math.sqrt(2.0) * factor_norm * legendre[degree] * cosine_terms[order_index]
                )
                basis_rows[centre - order_index] = (
                    math.sqrt(2.0) * factor_norm * legendre[degree] * sine_terms[order_index]
                )
    return jnp.stack(basis_rows)


def facing_table(normal_azimuth, normal_height, along_x, along_y, along_z):
    planar = jnp.sqrt(jnp.maximum(1.0 - normal_height * normal_height, 0.0))
    normal_x = planar * jnp.cos(normal_azimuth)
    normal_y = planar * jnp.sin(normal_azimuth)
    return jnp.maximum(
        along_x[:, None] * normal_x[None, :]
        + along_y[:, None] * normal_y[None, :]
        + along_z[:, None] * normal_height[None, :],
        0.0,
    )


def per_device(
    ray_code,
    occluder_list,
    list_count,
    normal_azimuth,
    normal_height,
    albedo,
    occluder_exit_radiance,
):
    dir_total, vertex_total = ray_code.shape
    blocks_held, coeff_total = (occluder_exit_radiance.shape[0], occluder_exit_radiance.shape[1])
    clusters, slot_total = occluder_list.shape
    own_cluster = lax.axis_index("cluster")
    first_dir = lax.axis_index("dir") * dir_total
    along_x, along_y, along_z = sphere_points(first_dir + lax.iota(jnp.int32, dir_total), NDIR)
    harmonics = harmonic_table(along_x, along_y, along_z, SHORD)
    facing = facing_table(normal_azimuth, normal_height, along_x, along_y, along_z)
    live_count = list_count[own_cluster]
    occluded = ray_code < live_count
    direct = jnp.dot(
        harmonics,
        jnp.where(occluded, 0.0, facing),
        precision=lax.Precision.HIGHEST,
        preferred_element_type=jnp.float32,
    )
    own_list = occluder_list[own_cluster]
    slot_index = lax.iota(jnp.int32, slot_total)
    portion_slice = lax.all_gather(occluder_exit_radiance, "cluster", axis=0, tiled=True)
    selected_entries = own_list[:, None] == lax.iota(jnp.int32, portion_slice.shape[0])[None, :]
    entries = jnp.einsum(
        "fx,xwn->fwn",
        selected_entries.astype(jnp.bfloat16),
        portion_slice,
        preferred_element_type=jnp.float32,
    ).astype(jnp.bfloat16)
    stacked = jnp.transpose(entries, (1, 0, 2)).reshape(coeff_total, slot_total * dir_total)
    block_width = min(512, vertex_total)
    block_count = vertex_total // block_width

    def one_block(block_index):
        first_vertex = block_index * block_width
        ray_codes = lax.dynamic_slice_in_dim(ray_code, first_vertex, block_width, 1)
        lit = lax.dynamic_slice_in_dim(facing, first_vertex, block_width, 1)
        weight = jnp.where(ray_codes < live_count, lit, 0.0)
        onehot = ray_codes[None, :, :] == slot_index[:, None, None]
        spread = (
            jnp.where(onehot, weight[None, :, :], 0.0)
            .astype(jnp.bfloat16)
            .reshape(slot_total * dir_total, block_width)
        )
        return jnp.dot(stacked, spread, preferred_element_type=jnp.float32)

    pieces = lax.map(one_block, lax.iota(jnp.int32, block_count))
    bounce = jnp.transpose(pieces, (1, 0, 2)).reshape(coeff_total, vertex_total)
    partial_sum = 4.0 * math.pi / NDIR * (direct + albedo[None, :] * bounce)
    summed = lax.psum_scatter(partial_sum, "dir", scatter_dimension=1, tiled=True)
    return summed.astype(jnp.bfloat16)


def solution(mesh):
    return jax.shard_map(
        per_device,
        mesh=mesh,
        in_specs=(
            P("dir", "cluster"),
            P(),
            P(),
            P("cluster"),
            P("cluster"),
            P("cluster"),
            P("cluster", None, "dir"),
        ),
        out_specs=P(None, ("cluster", "dir")),
        check_vma=False,
    )
```

profile of v0, /device:TPU:1, one launch (start us, length us, event | category | flops | bytes accessed | tf_op | source)
XLA Modules:
  0.0 316.4 jit_solution(9582630595501091377)
XLA Ops:
  12.7 4.3 %add_maximum_fusion = bf16[256,8192]{1,0:T(8,128)(2,1)} fusion(f32[8192]{0:T(1024)} %param.13, f32[256]{0:T(256)S(1)} %multiply_subtract_fusion, f32[8192]{0:T(1024)S(1)} %get-tuple-element.99, f32[256]{0:T(256)S(1)} %get-tuple-element.100, f32[8192]{0:T(1024)S(1)} %get-tuple-element.98, f32[256]{0:T(256)S(1)} %get-tuple-element.101), kind=kLoop, calls=%fused_computation.11 | loop fusion | flops 14680064 | bytes 4295680 | tf_op jit(solution)/shard_map/max | solution.py:67
  17.0 115.2 %all-gather.2.cloned.1.call-done = bf16[512,81,256]{2,0,1:T(8,128)(2,1)} async-done(((bf16[8,81,256]{2,0,1:T(8,128)(2,1)}), bf16[512,81,256]{2,0,1:T(8,128)(2,1)}) %all-gather.2.cloned.1.call-update) | async-done | bytes 21233680 | tf_op jit(solution)/shard_map/all_gather | solution.py:102
  132.1 10.0 %fusion.7 = bf16[81,16,256]{2,1,0:T(8,128)(2,1)S(1)} fusion(bf16[512,81,256]{2,0,1:T(8,128)(2,1)} %all-gather.2.cloned.1.call-done, s32[16]{0:T(128)S(1)} %dynamic-slice_reduce_fusion), kind=kOutput, calls=%fused_computation.16 | convolution fusion | flops 340078592 | bytes 21897280 | tf_op jit(solution)/shard_map/fx,xwn->fwn/dot_general | solution.py:104
  142.5 114.1 %while.12 = (s32[]{:T(128)}, f32[16,81,512]{2,1,0:T(8,128)}, s32[16]{0:T(128)S(1)}, s32[256,8192]{1,0:T(8,128)}, s32[]{:T(128)}, /*index=5*/bf16[256,8192]{1,0:T...) while((s32[]{:T(128)}, f32[16,81,512]{2,1,0:T(8,128)}, ...), condition=%wide.region_1.2_spmd.clone, body=%wide.region_0.1_spmd.clone.sunk | while | flops 344195072 | bytes 12181759 | solution.py:127
  143.8 1.8 dynamic-slice_select_fusion.2
  148.1 1.5 fusion.37
  151.0 1.8 dynamic-slice_select_fusion.2
  158.1 1.8 dynamic-slice_select_fusion.2
  165.2 1.8 dynamic-slice_select_fusion.2
  172.4 1.8 dynamic-slice_select_fusion.2
  176.6 1.5 fusion.37
  179.5 1.8 dynamic-slice_select_fusion.2
  186.6 1.8 dynamic-slice_select_fusion.2
  193.8 1.8 dynamic-slice_select_fusion.2
  198.0 1.5 fusion.37
  200.9 1.8 dynamic-slice_select_fusion.2
  208.0 1.8 dynamic-slice_select_fusion.2
  212.3 1.5 fusion.37
  215.2 1.8 dynamic-slice_select_fusion.2
  219.4 1.5 fusion.37
  222.3 1.8 dynamic-slice_select_fusion.2
  229.4 1.8 dynamic-slice_select_fusion.2
  236.6 1.8 dynamic-slice_select_fusion.2
  240.8 1.5 fusion.37
  243.7 1.8 dynamic-slice_select_fusion.2
  250.8 1.8 dynamic-slice_select_fusion.2
  255.1 1.5 fusion.37
  256.6 3.5 %copy.9 = f32[81,16,512]{2,1,0:T(8,128)S(1)} copy(f32[81,16,512]{2,0,1:T(8,128)} %bitcast.55) | data formatting | bytes 5308416 | tf_op jit(solution)/shard_map/transpose | solution.py:128
  260.6 2.0 copy.12
  262.7 9.5 %fusion.2 = f32[81,8192]{1,0:T(8,128)} fusion(f32[81,256]{1,0:T(8,128)S(1)} %stack.5, s32[256,8192]{1,0:T(8,128)S(1)} %bitcast.54, s32[]{:T(128)} %bitcast, f32[81,8192]{1,0:T(8,128)S(1)} %bitcast.56, f32[8192]{0:T(1024)S(1)} %copy-done.2, f32[8192]{0:T(1024)S(1)} %copy-done.1, f32[256]{0:T(256)S(1)} %multiply_subtract_fusion, ...), kind=kOutput, calls=%fused_computation.9 | convolution fusion | flops 2057199616 | bytes 13914116 | tf_op jit(solution)/shard_map/dot_general | solution.py:94
  272.2 35.5 %reduce-scatter.2.cloned.1.call-done = f32[81,2048]{1,0:T(8,128)} async-done(((f32[81,8192]{1,0:T(8,128)}), f32[81,2048]{1,0:T(8,128)}) %reduce-scatter.2.cloned.1.call-update) | async-done | bytes 663568 | tf_op jit(solution)/shard_map/reduce_scatter | solution.py:130
  307.7 1.9 convert_element_type.358
  (156 shorter events, 71.8 us)
Async XLA Ops:
  6.5 5.0 %copy-start = (s32[64,16]{0,1:T(8,128)S(1)}, s32[64,16]{0,1:T(8,128)}, u32[]{:S(2)}) copy-start(s32[64,16]{0,1:T(8,128)} %param.10) | copy-start | bytes 12292
  6.5 125.6 %all-gather.2.cloned.1.call-start = ((), (), s32[]{:S(2)}) async-start(), calls=%async_computation.1 | async-start | bytes 21565440 | tf_op jit(solution)/shard_map/all_gather | solution.py:102
  7.3 300.4 %reduce-scatter.2.cloned.1.call-start = ((), (), s32[]{:S(2)}) async-start(), calls=%async_computation.2 | async-start | bytes 3604480 | tf_op jit(solution)/shard_map/reduce_scatter | solution.py:130
  256.6 6.0 %slice-start = ((s8[8388608]{0:T(1024)(128)(4,1)}), s8[4194304]{0:T(1024)(128)(4,1)S(1)}, s32[]{:S(2)}) async-start(s8[8388608]{0:T(1024)(128)(4,1)} %bitcast.53), calls=%async_computation.3 | async-start | bytes 8388608
  256.6 6.0 %copy-start.1 = (f32[8192]{0:T(1024)S(1)}, f32[8192]{0:T(1024)}, u32[]{:S(2)}) copy-start(f32[8192]{0:T(1024)} %param.13) | copy-start | bytes 98308
  256.6 6.0 %copy-start.2 = (f32[8192]{0:T(1024)S(1)}, f32[8192]{0:T(1024)}, u32[]{:S(2)}) copy-start(f32[8192]{0:T(1024)} %param.14) | copy-start | bytes 98308
  260.1 2.5 slice-start.1
Sparse Core Ops, SparseCore 0:
  9.9 122.2 all-gather.1
  272.3 35.2 reduce-scatter.1
where the time goes:
time: 318 us; the launch traced here: 316 us
  waiting for transfers between devices  151 us (47%)
  other arithmetic  60.5 us (19%)
  matrix products  43.5 us (14%)
  local copies, waits for them, and re-layouts  37 us (12%)
  between operations  13.6 us (4%)
  loops' own time  10.4 us (3%)
    all_gather x1, waiting for transfers between devices, per_device(): lax.all_gather(occluder_exit_radiance, 'cluster', axis=0, tiled=True)  115 us
    reduce_scatter x1, waiting for transfers between devices, per_device(): lax.psum_scatter(partial_sum, 'dir', scatter_dimension=1, tiled=True)  35.5 us
    select_n x16, other arithmetic, one_block(): weight = jnp.where(ray_codes < live_count, lit, 0.0)  28.3 us
    dot_general x16, matrix products, one_block(): return jnp.dot(stacked, spread, preferred_element_type=jnp.float32)  24.1 us
    convert_element_type x16, other arithmetic, one_block(): spread = jnp.where(onehot, weight[None, :, :], 0.0).astype(jnp.bfloat16)....  22.4 us
    dynamic_slice x16, local copies, waits for them, and re-layouts, one_block(): ray_codes = lax.dynamic_slice_in_dim(ray_code, first_vertex, block_width, 1)  17.3 us
    another operation x1, loops' own time, per_device(): pieces = lax.map(one_block, lax.iota(jnp.int32, block_count))  10.4 us
    dynamic_slice x16, local copies, waits for them, and re-layouts, per_device(): pieces = lax.map(one_block, lax.iota(jnp.int32, block_count))  10.3 us
  transfers between devices with their start and end apart: 2, of which 2 were waited for; matrix products, arithmetic and copies ran while one was open for 3% of the time, Pallas kernels for 0%

commit v1 on v0

v1 whole, which is shorter than its diff:
```python
import functools
import math

import jax
import jax.numpy as jnp
import numpy as np
from jax import lax
from jax.experimental import pallas as pl
from jax.experimental.pallas import tpu as pltpu
from jax.sharding import PartitionSpec as P

NDIR = 1024
SHORD = 9
COEFFS = 81
SLOTS = 16
CLUSTERS = 64
BLK = 8
DIRS = 256
HALF = 128
VERTS = 8192
OWN = 2048
KG = 32
PARTS = 3
ROWS = KG * PARTS
SEND = 88
NB = 1024
NI = 256
F32 = jnp.float32
BF16 = jnp.bfloat16
MESH = pl.DeviceIdType.MESH
GOLDEN = math.pi * (3.0 - math.sqrt(5.0))


def direction_tables():
    p = np.arange(NDIR, dtype=np.float32)
    z = (np.float32(1.0) - (np.float32(2.0) * p + np.float32(1.0)) / np.float32(NDIR)).astype(np.float32)
    r = np.sqrt(np.maximum(np.float32(1.0) - z * z, np.float32(0.0)))
    t = (p * np.float32(GOLDEN)).astype(np.float64)
    x = (r * np.cos(t).astype(np.float32)).astype(np.float64)
    y = (r * np.sin(t).astype(np.float32)).astype(np.float64)
    z = z.astype(np.float64)
    c, s = [np.ones_like(x)], [np.zeros_like(x)]
    for _ in range(1, SHORD):
        c.append(c[-1] * x - s[-1] * y)
        s.append(c[-2] * y + s[-1] * x)
    rows = [None] * COEFFS
    for m in range(SHORD):
        q = [None] * SHORD
        q[m] = np.full_like(z, float(np.prod(np.arange(1, 2 * m, 2, dtype=np.float64))))
        if m + 1 < SHORD:
            q[m + 1] = z * (2 * m + 1) * q[m]
        for l in range(m + 2, SHORD):
            q[l] = ((2 * l - 1) * z * q[l - 1] - (l + m - 1) * q[l - 2]) / (l - m)
        for l in range(m, SHORD):
            n = math.sqrt((2 * l + 1) / (4.0 * math.pi) * math.factorial(l - m) / math.factorial(l + m))
            at = l * l + l
            if m == 0:
                rows[at] = n * q[l]
            else:
                rows[at + m] = math.sqrt(2.0) * n * q[l] * c[m]
                rows[at - m] = math.sqrt(2.0) * n * q[l] * s[m]
    table = np.zeros((4, ROWS, DIRS), np.float32)
    table[:, :COEFFS] = np.stack(rows).reshape(COEFFS, 4, DIRS).transpose(1, 0, 2)
    axes = np.zeros((4, DIRS, 8), np.float32)
    for i, a in enumerate((x, y, z)):
        axes[:, :, i] = a.reshape(4, DIRS)
    return table, axes


def place(cluster):
    chip = cluster // 2
    spread = (chip % 8) * 4 + chip // 8
    return cluster % 2, (spread * 5) % KG


def fetch_kernel(block_ref, list_ref, out_ref, slices, picked, table, send1, recv1, send2, recv2):
    me = lax.axis_index("cluster")
    my_half, my_group = place(me)
    barrier = pltpu.get_barrier_semaphore()

    def greet(i, carry):
        pl.semaphore_signal(
            barrier, inc=1, device_id={"cluster": (me + i) % CLUSTERS}, device_id_type=MESH
        )
        return carry

    lax.fori_loop(1, CLUSTERS, greet, 0)
    slices[me] = block_ref[my_half, my_group]
    pl.semaphore_wait(barrier, CLUSTERS - 1)

    def first(i):
        peer = (me + i) % CLUSTERS
        half, group = place(peer)
        return pltpu.make_async_remote_copy(
            src_ref=block_ref.at[half, group],
            dst_ref=slices.at[me],
            send_sem=send1,
            recv_sem=recv1,
            device_id={"cluster": peer},
            device_id_type=MESH,
        )

    def start_first(i, carry):
        first(i).start()
        return carry

    lax.fori_loop(1, CLUSTERS, start_first, 0)
    chosen = jnp.where(
        list_ref[...] == lax.broadcasted_iota(jnp.int32, (CLUSTERS * SLOTS, CLUSTERS * BLK), 1), 1.0, 0.0
    ).astype(BF16)
    others = slices.at[pl.ds(0, CLUSTERS - 1)]
    pltpu.make_async_copy(others, others, recv1).wait()
    for part in range(PARTS):
        held = slices[:, part].reshape(CLUSTERS * BLK, HALF)
        rows = jnp.dot(chosen, held, preferred_element_type=F32).astype(BF16)
        picked[:, part] = rows.reshape(CLUSTERS, SLOTS, HALF)
    table[my_half, my_group] = picked[me]

    def second(i):
        peer = (me + i) % CLUSTERS
        return pltpu.make_async_remote_copy(
            src_ref=picked.at[peer],
            dst_ref=table.at[my_half, my_group],
            send_sem=send2,
            recv_sem=recv2,
            device_id={"cluster": peer},
            device_id_type=MESH,
        )

    def start_second(i, carry):
        second(i).start()
        return carry

    lax.fori_loop(1, CLUSTERS, start_second, 0)
    to = lax.broadcasted_iota(jnp.int32, (SLOTS * KG, SLOTS * KG), 0)
    fro = lax.broadcasted_iota(jnp.int32, (SLOTS * KG, SLOTS * KG), 1)
    turn = jnp.where((to % KG) * SLOTS + to // KG == fro, 1.0, 0.0).astype(BF16)
    pltpu.make_async_copy(others, others, send1).wait()
    sent = picked.at[pl.ds(0, CLUSTERS - 1)]
    pltpu.make_async_copy(sent, sent, send2).wait()
    pltpu.make_async_copy(sent, sent, recv2).wait()
    for part in range(PARTS):
        for half in range(2):
            got = table[half, :, part].reshape(KG * SLOTS, HALF)
            turned = jnp.dot(turn, got, preferred_element_type=F32).astype(BF16)
            out_ref[:, part * KG : (part + 1) * KG, half * HALF : (half + 1) * HALF] = turned.reshape(
                SLOTS, KG, HALF
            )


def compute_kernel(
    code_ref, count_ref, axes_ref, vert_ref, harm_ref, table_ref, out_ref,
    codes, total, parts, got, code_sem, send_sem, recv_sem,
):
    me = lax.axis_index("dir")
    cluster = lax.axis_index("cluster")
    steps = VERTS // NB
    per = OWN // NB

    def first_of(t):
        return pl.multiple_of(((me + 1 + t // per) % 4) * OWN + (t % per) * NB, NB)

    def fetch(t):
        return pltpu.make_async_copy(code_ref.at[:, pl.ds(first_of(t), NB)], codes.at[t], code_sem.at[t])

    for t in range(steps):
        fetch(t).start()
    barrier = pltpu.get_barrier_semaphore()
    for i in range(1, 4):
        pl.semaphore_signal(barrier, inc=1, device_id={"dir": (me + i) % 4}, device_id_type=MESH)
    pl.semaphore_wait(barrier, 3)
    count = count_ref[cluster]
    x, y, z = (axes_ref[me, :, i : i + 1] for i in range(3))

    def exchange(t):
        owner = t // per
        return pltpu.make_async_remote_copy(
            src_ref=parts.at[t],
            dst_ref=got.at[t],
            send_sem=send_sem.at[t],
            recv_sem=recv_sem.at[t],
            device_id={"dir": (me + 1 + owner) % 4},
            device_id_type=MESH,
        )

    def step(t, carry):
        fetch(t).wait()
        base = first_of(t)
        for n in range(NB // NI):
            cols = slice(n * NI, (n + 1) * NI)
            vert = vert_ref[:, pl.ds(pl.multiple_of(base + n * NI, NI), NI)]
            code = codes[t, :, cols]
            facing = jnp.maximum(x * vert[0:1] + y * vert[1:2] + z * vert[2:3], 0.0)
            hit = code < count
            lit = jnp.where(hit, 0.0, facing).astype(BF16)
            weight = facing.astype(BF16)
            slot = jnp.where(hit, code, SLOTS).astype(jnp.int16)
            bounce = None
            for s in range(SLOTS):
                spread = jnp.where(slot == jnp.int16(s), weight, jnp.zeros_like(weight))
                term = jnp.dot(table_ref[s], spread, preferred_element_type=F32)
                bounce = term if bounce is None else bounce + term
            direct = jnp.dot(harm_ref[me], lit, preferred_element_type=F32)
            total[t % per, :, cols] = (4.0 * math.pi / NDIR) * (direct + vert[3:4] * bounce)

        @pl.when(t < steps - per)
        def _():
            parts[t] = total[t % per, :SEND].astype(BF16)
            exchange(t).start()

        return carry

    lax.fori_loop(0, steps, step, 0)
    for t in range(steps - per):
        exchange(t).wait()
    for h in range(per):
        mine = total[h, :SEND]
        for i in range(3):
            mine = mine + got[i * per + h].astype(F32)
        out_ref[:, h * NB : (h + 1) * NB] = mine[:COEFFS].astype(BF16)


def per_device(
    ray_code, occluder_list, list_count, normal_azimuth, normal_height, albedo, occluder_exit_radiance
):
    table, axes = direction_tables()
    blocks = jnp.pad(occluder_exit_radiance, ((0, 0), (0, ROWS - COEFFS), (0, 0)))
    blocks = blocks.reshape(BLK, PARTS, KG, 2, HALF).transpose(3, 2, 1, 0, 4)
    planar = jnp.sqrt(jnp.maximum(1.0 - normal_height * normal_height, 0.0))
    verts = jnp.stack(
        [planar * jnp.cos(normal_azimuth), planar * jnp.sin(normal_azimuth), normal_height, albedo]
    )
    vmem = pl.BlockSpec(memory_space=pltpu.VMEM)
    tables = pl.pallas_call(
        fetch_kernel,
        out_shape=jax.ShapeDtypeStruct((SLOTS, ROWS, DIRS), BF16),
        in_specs=[vmem, vmem],
        out_specs=vmem,
        scratch_shapes=[
            pltpu.VMEM((CLUSTERS, PARTS, BLK, HALF), BF16),
            pltpu.VMEM((CLUSTERS, PARTS, SLOTS, HALF), BF16),
            pltpu.VMEM((2, KG, PARTS, SLOTS, HALF), BF16),
            pltpu.SemaphoreType.DMA,
            pltpu.SemaphoreType.DMA,
            pltpu.SemaphoreType.DMA,
            pltpu.SemaphoreType.DMA,
        ],
        compiler_params=pltpu.CompilerParams(
            collective_id=0, has_side_effects=True, vmem_limit_bytes=32 << 20
        ),
        name="fetch",
    )(blocks, occluder_list.reshape(CLUSTERS * SLOTS, 1))
    steps, per = VERTS // NB, OWN // NB
    return pl.pallas_call(
        compute_kernel,
        out_shape=jax.ShapeDtypeStruct((COEFFS, OWN), BF16),
        in_specs=[
            pl.BlockSpec(memory_space=pl.ANY),
            pl.BlockSpec(memory_space=pltpu.SMEM),
            vmem, vmem, vmem, vmem,
        ],
        out_specs=vmem,
        scratch_shapes=[
            pltpu.VMEM((steps, DIRS, NB), jnp.int32),
            pltpu.VMEM((per, ROWS, NB), F32),
            pltpu.VMEM((steps - per, SEND, NB), BF16),
            pltpu.VMEM((steps - per, SEND, NB), BF16),
            pltpu.SemaphoreType.DMA((steps,)),
            pltpu.SemaphoreType.DMA((steps - per,)),
            pltpu.SemaphoreType.DMA((steps - per,)),
        ],
        compiler_params=pltpu.CompilerParams(
            collective_id=1, has_side_effects=True, vmem_limit_bytes=56 << 20
        ),
        name="transfer",
    )(ray_code, list_count, jnp.asarray(axes), verts, jnp.asarray(table).astype(BF16), tables)


def solution(mesh):
    return jax.shard_map(
        per_device,
        mesh=mesh,
        in_specs=(
            P("dir", "cluster"),
            P(),
            P(),
            P("cluster"),
            P("cluster"),
            P("cluster"),
            P("cluster", None, "dir"),
        ),
        out_specs=P(None, ("cluster", "dir")),
        check_vma=False,
    )
```

time: 318 us -> 80.1 us (0.25)
  waiting for transfers between devices: 151 us -> 0 us
  Pallas kernels: 0 us -> 72.4 us
  other arithmetic: 60.5 us -> 2.48 us
  matrix products: 43.5 us -> 0 us
  local copies, waits for them, and re-layouts: 37 us -> 4.83 us
  between operations: 13.6 us -> 0.05 us
  loops' own time: 10.4 us -> 0 us
    all_gather x1 -> x0, waiting for transfers between devices: 115 us -> none  [per_device(): lax.all_gather(occluder_exit_radiance, 'cluster', axis=0, tiled=True)]
    pallas_call x0 -> x2, Pallas kernels: none -> 72.4 us  [the longest x1 45 us: per_device(): pl.pallas_call(fetch_kernel, out_shape=jax.ShapeDtypeStruct((SLOTS, ROWS,...]
    dot_general x18 -> x0, matrix products: 43.5 us -> none  [the longest x16 24.1 us: one_block(): return jnp.dot(stacked, spread, preferred_element_type=jnp.float32)]
    reduce_scatter x1 -> x0, waiting for transfers between devices: 35.5 us -> none  [per_device(): lax.psum_scatter(partial_sum, 'dir', scatter_dimension=1, tiled=True)]
    dynamic_slice x34 -> x0, local copies, waits for them, and re-layouts: 29.1 us -> none  [the longest x16 17.3 us: one_block(): ray_codes = lax.dynamic_slice_in_dim(ray_code, first_vertex, block_width, 1)]
    select_n x16 -> x0, other arithmetic: 28.3 us -> none  [one_block(): weight = jnp.where(ray_codes < live_count, lit, 0.0)]
    convert_element_type x17 -> x0, other arithmetic: 24.3 us -> none  [the longest x16 22.4 us: one_block(): spread = jnp.where(onehot, weight[None, :, :], 0.0).astype(jnp.bfloat16)....]
    another operation x1 -> x0, loops' own time: 10.4 us -> none  [per_device(): pieces = lax.map(one_block, lax.iota(jnp.int32, block_count))]
  transfers between devices with their start and end apart: 2 -> 0, of which waited for: 2 -> 0; matrix products, arithmetic and copies ran while one was open for 3% -> 0% of each run, Pallas kernels for 0% -> 0%
where the time goes in v1:
time: 80.1 us; the launch traced here: 79.8 us
  Pallas kernels  72.4 us (90%)
  local copies, waits for them, and re-layouts  4.83 us (6%)
  other arithmetic  2.48 us (3%)
    pallas_call x1, Pallas kernels, per_device(): pl.pallas_call(fetch_kernel, out_shape=jax.ShapeDtypeStruct((SLOTS, ROWS,...  45 us
    pallas_call x1, Pallas kernels, per_device(): pl.pallas_call(compute_kernel, out_shape=jax.ShapeDtypeStruct((COEFFS, OW...  27.4 us
    unnamed x4, local copies, waits for them, and re-layouts  3.39 us

profile of v1, /device:TPU:1, one launch (start us, length us, event | category | flops | bytes accessed | tf_op | source)
XLA Modules:
  0.0 79.8 jit_solution(1242181388522041522)
XLA Ops:
  0.0 0.8 copy.13
  0.8 0.9 %cosine_multiply_fusion = (f32[8192]{0:T(1024)S(1)}, f32[8192]{0:T(1024)S(1)}) fusion(f32[8192]{0:T(1024)} %param.12, f32[8192]{0:T(1024)} %param.13), kind=kLoop, calls=%fused_computation.3 | loop fusion | flops 40960 | bytes 131072 | tf_op jit(solution)/shard_map/mul | solution.py:231
  1.7 1.6 %pad_maximum_fusion.vert_ref = f32[4,8192]{1,0:T(4,128)} fusion(f32[1,8192]{1,0:T(1,128)} %bitcast.13, f32[1,8192]{1,0:T(1,128)} %bitcast.10, f32[1,8192]{1,0:T(1,128)S(1)} %bitcast.12, f32[1,8192]{1,0:T(1,128)S(1)} %bitcast.11), kind=kLoop, calls=%fused_computation.1 | loop fusion | flops 98304 | bytes 262144 | tf_op jit(solution)/shard_map/stack | solution.py:230
  3.3 1.0 %pad.4 = bf16[8,96,256]{2,0,1:T(8,128)(2,1)S(1)} pad(bf16[8,81,256]{2,0,1:T(8,128)(2,1)} %param.15, bf16[]{:T(256)} %constant.10.clone.1), padding=0_0x0_15x0_0 | pad | bytes 724994 | tf_op jit(solution)/shard_map/jit(_pad)/pad | solution.py:227
  4.3 0.1 reshape.8
  4.4 0.1 copy.18
  4.4 0.3 reshape.9.list_ref
  4.7 45.0 %fetch.1.table_ref = bf16[16,96,256]{2,1,0:T(8,128)(2,1)S(1)} custom-call(bf16[2,32,3,8,128]{4,3,2,1,0:T(8,128)(2,1)S(1)} %bitcast.9, s32[1024,1]{1,0:T(8,128)S(1)} %reshape.9.list_ref), custom_call_target="tpu_custom_call" | custom-call | tf_op jit(solution)/shard_map/fetch/pallas_call | solution.py:234
  49.7 0.0 copy-start
  49.7 0.9 %copy-done = bf16[16,96,256]{2,1,0:T(8,128)(2,1)} copy-done((bf16[16,96,256]{2,1,0:T(8,128)(2,1)}, bf16[16,96,256]{2,1,0:T(8,128)(2,1)S(1)}, u32[]{:S(2)}) %copy-start) | copy-done | bytes 786456
  50.6 27.4 %transfer.1 = bf16[81,2048]{1,0:T(8,128)(2,1)} custom-call(s32[256,8192]{1,0:T(8,128)} %code_ref.1, s32[64]{0:T(128)} %count_ref.1, f32[4,256,8]{2,1,0:T(8,128)} %constant.11.clone.axes_ref, f32[4,8192]{1,0:T(4,128)} %pad_maximum_fusion.vert_ref, bf16[4,96,256]{2,1,0:T(8,128)(2,1)} %constant.16.harm_ref, bf16[16,96,256]{2,1,0:T(8,128)(2,1)} %copy-done), custom_call_target="tpu_custom_call" | custom-call | tf_op jit(solution)/shard_map/transfer/pallas_call | solution.py:254
  78.0 1.7 %copy.20 = bf16[81,2048]{1,0:T(8,128)(2,1)} copy(bf16[81,2048]{1,0:T(8,128)(2,1)} %transfer.1) | data formatting | bytes 663552
Async XLA Ops:
  49.7 0.9 %copy-start = (bf16[16,96,256]{2,1,0:T(8,128)(2,1)}, bf16[16,96,256]{2,1,0:T(8,128)(2,1)S(1)}, u32[]{:S(2)}) copy-start(bf16[16,96,256]{2,1,0:T(8,128)(2,1)S(1)} %fetch.1.table_ref) | copy-start | bytes 2359300

commit v2 on v1

v2 whole, which is shorter than its diff:
```python
import math

import jax
import jax.numpy as jnp
import numpy as np
from jax import lax
from jax.experimental import pallas as pl
from jax.experimental.pallas import tpu as pltpu
from jax.sharding import PartitionSpec as P

NDIR = 1024
SHORD = 9
COEFFS = 81
SLOTS = 16
CLUSTERS = 64
BLK = 8
DIRS = 256
HALF = 128
VERTS = 8192
OWN = 2048
KG = 32
PARTS = 3
ROWS = KG * PARTS
SEND = 88
FULL = COEFFS - KG * (PARTS - 1)
NB = 1024
NI = 256
F32 = jnp.float32
BF16 = jnp.bfloat16
MESH = pl.DeviceIdType.MESH
SCALE = 4.0 * math.pi / NDIR
GOLDEN = math.pi * (3.0 - math.sqrt(5.0))


def direction_tables():
    p = np.arange(NDIR, dtype=np.float32)
    z = (np.float32(1.0) - (np.float32(2.0) * p + np.float32(1.0)) / np.float32(NDIR)).astype(np.float32)
    r = np.sqrt(np.maximum(np.float32(1.0) - z * z, np.float32(0.0)))
    t = (p * np.float32(GOLDEN)).astype(np.float64)
    x = (r * np.cos(t).astype(np.float32)).astype(np.float64)
    y = (r * np.sin(t).astype(np.float32)).astype(np.float64)
    z = z.astype(np.float64)
    c, s = [np.ones_like(x)], [np.zeros_like(x)]
    for _ in range(1, SHORD):
        c.append(c[-1] * x - s[-1] * y)
        s.append(c[-2] * y + s[-1] * x)
    rows = [None] * COEFFS
    for m in range(SHORD):
        q = [None] * SHORD
        q[m] = np.full_like(z, float(np.prod(np.arange(1, 2 * m, 2, dtype=np.float64))))
        if m + 1 < SHORD:
            q[m + 1] = z * (2 * m + 1) * q[m]
        for l in range(m + 2, SHORD):
            q[l] = ((2 * l - 1) * z * q[l - 1] - (l + m - 1) * q[l - 2]) / (l - m)
        for l in range(m, SHORD):
            n = math.sqrt((2 * l + 1) / (4.0 * math.pi) * math.factorial(l - m) / math.factorial(l + m))
            at = l * l + l
            if m == 0:
                rows[at] = n * q[l]
            else:
                rows[at + m] = math.sqrt(2.0) * n * q[l] * c[m]
                rows[at - m] = math.sqrt(2.0) * n * q[l] * s[m]
    table = np.zeros((4, ROWS, DIRS), np.float32)
    table[:, :COEFFS] = np.stack(rows).reshape(COEFFS, 4, DIRS).transpose(1, 0, 2)
    axes = np.zeros((4, DIRS, 8), np.float32)
    for i, a in enumerate((x, y, z)):
        axes[:, :, i] = a.reshape(4, DIRS)
    return table, axes


def place(cluster):
    chip = lax.div(cluster, 2)
    spread = lax.rem(chip, 8) * 4 + lax.div(chip, 8)
    return lax.rem(cluster, 2), lax.rem(spread * 5, KG)


def transfer_kernel(
    code_ref, count_ref, block_ref, list_ref, axes_ref, azimuth_ref, height_ref, albedo_ref, harm_ref, out_ref,
    codes, weight, slot, direct, total, normal, chosen, turn, slices, picked, table, matrix, parts, got,
    code_sem, send_a, send_b, recv_a, recv_b, send_c, send_d, recv_c, recv_d, send_sem, recv_sem,
):
    me = lax.axis_index("cluster")
    row = lax.axis_index("dir")
    my_half, my_group = place(me)
    steps = VERTS // NB

    def first_of(t):
        pair, half = lax.div(t, 2), lax.rem(t, 2)
        ahead = lax.rem(2 + pair, 4) + lax.div(pair, 2) * (1 - 2 * lax.rem(pair, 2))
        ahead = ahead + 2 * half * lax.rem(lax.div(pair + 1, 2), 2)
        return pl.multiple_of(lax.rem(row + ahead, 4) * OWN + half * NB, NB)

    def fetch(t):
        return pltpu.make_async_copy(code_ref.at[:, pl.ds(first_of(t), NB)], codes.at[t], code_sem.at[t])

    def start_fetch(t, carry):
        fetch(t).start()
        return carry

    lax.fori_loop(0, steps, start_fetch, 0)
    barrier = pltpu.get_barrier_semaphore()

    def greet(i, carry):
        pl.semaphore_signal(
            barrier, inc=1, device_id={"cluster": lax.rem(me + i, CLUSTERS)}, device_id_type=MESH
        )
        return carry

    lax.fori_loop(1, CLUSTERS, greet, 0)
    for i in (1, 3):
        pl.semaphore_signal(barrier, inc=1, device_id={"dir": lax.rem(row + i, 4)}, device_id_type=MESH)

    slices[me] = block_ref[my_half, my_group]
    chosen[...] = jnp.where(
        list_ref[...] == lax.broadcasted_iota(jnp.int32, (CLUSTERS * SLOTS, CLUSTERS * BLK), 1), 1.0, 0.0
    ).astype(BF16)
    to = lax.broadcasted_iota(jnp.int32, (SLOTS * KG, SLOTS * KG), 0)
    fro = lax.broadcasted_iota(jnp.int32, (SLOTS * KG, SLOTS * KG), 1)
    turn[...] = jnp.where((to % KG) * SLOTS + to // KG == fro, 1.0, 0.0).astype(BF16)
    table[:, FULL:, PARTS - 1] = jnp.zeros((2, KG - FULL, SLOTS, HALF), BF16)
    height = height_ref[...]
    planar = jnp.sqrt(jnp.maximum(1.0 - height * height, 0.0))
    normal[0] = planar * jnp.cos(azimuth_ref[...])
    normal[1] = planar * jnp.sin(azimuth_ref[...])
    pl.semaphore_wait(barrier, CLUSTERS + 1)

    def first(i, lead):
        peer = lax.rem(me + i, CLUSTERS)
        half, group = place(peer)
        units = pl.ds(0, PARTS - 1) if lead else pl.ds(PARTS - 1, 1)
        return group, pltpu.make_async_remote_copy(
            src_ref=block_ref.at[half, group, units],
            dst_ref=slices.at[me, units],
            send_sem=send_a if lead else send_b,
            recv_sem=recv_a if lead else recv_b,
            device_id={"cluster": peer},
            device_id_type=MESH,
        )

    def start_first(i, carry):
        first(i, True)[1].start()
        return carry

    def start_first_rest(i, carry):
        group, copy = first(i, False)

        @pl.when(group < FULL)
        def _():
            copy.start()

        return carry

    lax.fori_loop(1, CLUSTERS, start_first, 0)
    lax.fori_loop(1, CLUSTERS, start_first_rest, 0)

    count = count_ref[me]
    x, y, z = (axes_ref[row, :, i : i + 1] for i in range(3))

    def across(ref, at):
        return jnp.concatenate([ref[pl.ds(at + i, 1), :] for i in range(NI // HALF)], axis=1)

    def prepare(t, carry):
        fetch(t).wait()
        base = lax.div(first_of(t), HALF)
        for n in range(NB // NI):
            cols = slice(n * NI, (n + 1) * NI)
            at = base + n * (NI // HALF)
            code = codes[t, :, cols]
            facing = jnp.maximum(
                x * across(normal.at[0], at) + y * across(normal.at[1], at) + z * across(height_ref, at), 0.0
            )
            hit = code < count
            weight[t, :, cols] = facing.astype(BF16)
            slot[t, :, cols] = jnp.where(hit, code, SLOTS).astype(jnp.int16)
            lit = jnp.where(hit, 0.0, facing)
            high = lit.astype(BF16)
            low = (lit - high.astype(F32)).astype(BF16)
            both = jnp.dot(harm_ref[row], high, preferred_element_type=F32)
            rest = jnp.dot(harm_ref[row, :ROWS], low, preferred_element_type=F32)
            direct[t, :, cols] = SCALE * (both[:ROWS] + both[ROWS:] + rest)
        return carry

    lax.fori_loop(0, 4, prepare, 0)

    others = slices.at[pl.ds(0, CLUSTERS - 1), pl.ds(0, PARTS - 1)]
    pltpu.make_async_copy(others, others, recv_a).wait()
    held = jnp.concatenate([slices[:, i].reshape(CLUSTERS * BLK, HALF) for i in range(PARTS - 1)], axis=1)
    rows = jnp.dot(chosen[...], held, preferred_element_type=F32).astype(BF16)
    for i in range(PARTS - 1):
        picked[:, i] = rows[:, i * HALF : (i + 1) * HALF].reshape(CLUSTERS, SLOTS, HALF)

    def second(i, lead):
        peer = lax.rem(me + i, CLUSTERS)
        units = pl.ds(0, PARTS - 1) if lead else pl.ds(PARTS - 1, 1)
        return pltpu.make_async_remote_copy(
            src_ref=picked.at[peer, units],
            dst_ref=table.at[my_half, my_group, units],
            send_sem=send_c if lead else send_d,
            recv_sem=recv_c if lead else recv_d,
            device_id={"cluster": peer},
            device_id_type=MESH,
        )

    def start_second(i, carry):
        second(i, True).start()
        return carry

    def start_second_rest(i, carry):
        second(i, False).start()
        return carry

    lax.fori_loop(1, CLUSTERS, start_second, 0)
    table[my_half, my_group, : PARTS - 1] = picked[me, : PARTS - 1]
    last = slices.at[pl.ds(0, CLUSTERS - 1), pl.ds(PARTS - 1, 1)]

    @pl.when(my_group < FULL)
    def _():
        pltpu.make_async_copy(last, last, recv_b).wait()
        held = slices[:, PARTS - 1].reshape(CLUSTERS * BLK, HALF)
        rows = jnp.dot(chosen[...], held, preferred_element_type=F32).astype(BF16)
        picked[:, PARTS - 1] = rows.reshape(CLUSTERS, SLOTS, HALF)
        lax.fori_loop(1, CLUSTERS, start_second_rest, 0)
        table[my_half, my_group, PARTS - 1] = picked[me, PARTS - 1]

    lax.fori_loop(4, steps, prepare, 0)

    pltpu.make_async_copy(others, others, send_a).wait()
    sent = picked.at[pl.ds(0, CLUSTERS - 1), pl.ds(0, PARTS - 1)]
    tail = picked.at[pl.ds(0, CLUSTERS - 1), pl.ds(PARTS - 1, 1)]
    pltpu.make_async_copy(sent, sent, send_c).wait()

    @pl.when(my_group < FULL)
    def _():
        fewer = slices.at[pl.ds(0, 2 * FULL - 1), pl.ds(PARTS - 1, 1)]
        pltpu.make_async_copy(fewer, fewer, send_b).wait()
        pltpu.make_async_copy(tail, tail, send_d).wait()
        less = picked.at[pl.ds(0, 2 * FULL - 1), pl.ds(PARTS - 1, 1)]
        pltpu.make_async_copy(less, less, recv_d).wait()

    @pl.when(my_group >= FULL)
    def _():
        fewer = slices.at[pl.ds(0, 2 * FULL), pl.ds(PARTS - 1, 1)]
        pltpu.make_async_copy(fewer, fewer, send_b).wait()
        less = picked.at[pl.ds(0, 2 * FULL), pl.ds(PARTS - 1, 1)]
        pltpu.make_async_copy(less, less, recv_d).wait()

    pltpu.make_async_copy(sent, sent, recv_c).wait()
    for i in range(PARTS):
        both = jnp.concatenate([table[h, :, i].reshape(KG * SLOTS, HALF) for h in range(2)], axis=1)
        turned = jnp.dot(turn[...], both, preferred_element_type=F32).astype(BF16)
        matrix[:, i * KG : (i + 1) * KG, :] = turned.reshape(SLOTS, KG, DIRS)

    def exchange(t):
        way = (1 - 2 * lax.rem(t, 2)) * (1 - 2 * lax.rem(lax.div(t, 2), 2))
        return pltpu.make_async_remote_copy(
            src_ref=parts.at[t],
            dst_ref=got.at[t],
            send_sem=send_sem.at[t],
            recv_sem=recv_sem.at[t],
            device_id={"dir": lax.rem(row + way + 4, 4)},
            device_id_type=MESH,
        )

    def step(t, carry):
        base = lax.div(first_of(t), HALF)
        for n in range(NB // NI):
            cols = slice(n * NI, (n + 1) * NI)
            held, code = weight[t, :, cols], slot[t, :, cols]
            bounce = None
            for s in range(SLOTS):
                spread = jnp.where(code == jnp.int16(s), held, jnp.zeros_like(held))
                term = jnp.dot(matrix[s], spread, preferred_element_type=F32)
                bounce = term if bounce is None else bounce + term
            gain = SCALE * across(albedo_ref, base + n * (NI // HALF))
            total[:, cols] = direct[t, :, cols] + gain * bounce

        @pl.when(t < 4)
        def _():
            parts[t] = total[:SEND].astype(BF16)
            exchange(t).start()

        @pl.when(lax.div(t, 2) == 2)
        def _():
            exchange(t - 4).wait_recv()
            parts[t] = (total[:SEND] + got[t - 4].astype(F32)).astype(BF16)
            exchange(t).start()

        @pl.when(t >= 6)
        def _():
            exchange(t - 4).wait_recv()
            exchange(t - 2).wait_recv()
            mine = total[:SEND] + got[t - 4].astype(F32) + got[t - 2].astype(F32)
            out_ref[:, pl.ds(pl.multiple_of((t - 6) * NB, NB), NB)] = mine[:COEFFS].astype(BF16)

        return carry

    lax.fori_loop(0, steps, step, 0)
    for t in range(steps - 2):
        exchange(t).wait_send()


def per_device(
    ray_code, occluder_list, list_count, normal_azimuth, normal_height, albedo, occluder_exit_radiance
):
    harmonics, axes = direction_tables()
    high = harmonics.astype(BF16)
    harmonics = np.concatenate([high, (harmonics - high.astype(np.float32)).astype(BF16)], axis=1)
    blocks = jnp.pad(occluder_exit_radiance, ((0, 0), (0, ROWS - COEFFS), (0, 0)))
    blocks = blocks.reshape(BLK, PARTS, KG, 2, HALF).transpose(3, 2, 1, 0, 4)
    vmem = pl.BlockSpec(memory_space=pltpu.VMEM)
    steps = VERTS // NB
    by_lane = (VERTS // HALF, HALF)
    dma = pltpu.SemaphoreType.DMA
    return pl.pallas_call(
        transfer_kernel,
        out_shape=jax.ShapeDtypeStruct((COEFFS, OWN), BF16),
        in_specs=[
            pl.BlockSpec(memory_space=pl.ANY),
            pl.BlockSpec(memory_space=pltpu.SMEM),
        ]
        + [vmem] * 7,
        out_specs=vmem,
        scratch_shapes=[
            pltpu.VMEM((steps, DIRS, NB), jnp.int32),
            pltpu.VMEM((steps, DIRS, NB), BF16),
            pltpu.VMEM((steps, DIRS, NB), jnp.int16),
            pltpu.VMEM((steps, ROWS, NB), F32),
            pltpu.VMEM((ROWS, NB), F32),
            pltpu.VMEM((2,) + by_lane, F32),
            pltpu.VMEM((CLUSTERS * SLOTS, CLUSTERS * BLK), BF16),
            pltpu.VMEM((SLOTS * KG, SLOTS * KG), BF16),
            pltpu.VMEM((CLUSTERS, PARTS, BLK, HALF), BF16),
            pltpu.VMEM((CLUSTERS, PARTS, SLOTS, HALF), BF16),
            pltpu.VMEM((2, KG, PARTS, SLOTS, HALF), BF16),
            pltpu.VMEM((SLOTS, ROWS, DIRS), BF16),
            pltpu.VMEM((steps - 2, SEND, NB), BF16),
            pltpu.VMEM((steps - 2, SEND, NB), BF16),
            dma((steps,)),
        ]
        + [dma] * 8
        + [dma((steps - 2,)), dma((steps - 2,))],
        compiler_params=pltpu.CompilerParams(
            collective_id=0, has_side_effects=True, vmem_limit_bytes=60 << 20
        ),
        name="transfer",
    )(
        ray_code,
        list_count,
        blocks,
        occluder_list.reshape(CLUSTERS * SLOTS, 1),
        jnp.asarray(axes),
        normal_azimuth.reshape(by_lane),
        normal_height.reshape(by_lane),
        albedo.reshape(by_lane),
        jnp.asarray(harmonics),
    )


def solution(mesh):
    return jax.shard_map(
        per_device,
        mesh=mesh,
        in_specs=(
            P("dir", "cluster"),
            P(),
            P(),
            P("cluster"),
            P("cluster"),
            P("cluster"),
            P("cluster", None, "dir"),
        ),
        out_specs=P(None, ("cluster", "dir")),
        check_vma=False,
    )
```

time: 80.1 us -> 68.2 us (0.85)
  Pallas kernels: 72.4 us -> 62.4 us
  other arithmetic: 2.48 us -> 0 us
    pallas_call x2 -> x1, Pallas kernels: 72.4 us -> 62.4 us  [per_device(): pl.pallas_call(transfer_kernel, out_shape=jax.ShapeDtypeStruct((COEFFS, O...]
    another operation x1 -> x0, other arithmetic: 1.56 us -> none  [per_device(): jnp.stack([planar * jnp.cos(normal_azimuth), planar * jnp.sin(normal_azim...]
    mul x1 -> x0, other arithmetic: 0.91 us -> none  [per_device(): planar * jnp.cos(normal_azimuth)]
    unnamed x4 -> x2, local copies, waits for them, and re-layouts: 3.39 us -> 2.52 us
where the time goes in v2:
time: 68.2 us; the launch traced here: 68 us
  Pallas kernels  62.4 us (91%)
  local copies, waits for them, and re-layouts  5.52 us (8%)
    pallas_call x1, Pallas kernels, per_device(): pl.pallas_call(transfer_kernel, out_shape=jax.ShapeDtypeStruct((COEFFS, O...  62.4 us
    unnamed x2, local copies, waits for them, and re-layouts  2.52 us

profile of v2, /device:TPU:1, one launch (start us, length us, event | category | flops | bytes accessed | tf_op | source)
XLA Modules:
  0.0 68.0 jit_solution(3839583439250854120)
XLA Ops:
  0.0 0.8 %copy.13 = s32[64,16]{1,0:T(8,128)S(1)} copy(s32[64,16]{0,1:T(8,128)} %param.10) | data formatting | bytes 8192 | tf_op args[1]
  0.8 1.0 %pad.4 = bf16[8,96,256]{2,0,1:T(8,128)(2,1)S(1)} pad(bf16[8,81,256]{2,0,1:T(8,128)(2,1)} %param.15, bf16[]{:T(256)} %constant.6.clone.1), padding=0_0x0_15x0_0 | pad | bytes 724994 | tf_op jit(solution)/shard_map/jit(_pad)/pad | solution.py:308
  1.8 0.1 reshape.20
  1.9 0.8 %copy.18 = bf16[8,3,32,2,128]{4,0,1,2,3:T(8,128)(2,1)} copy(bf16[8,3,32,2,128]{4,3,0,2,1:T(2,128)(2,1)S(1)} %reshape.20) | data formatting | bytes 786432 | tf_op jit(solution)/shard_map/reshape | solution.py:309
  2.7 1.1 %reshape.21.list_ref = s32[1024,1]{1,0:T(8,128)} reshape(s32[64,16]{1,0:T(8,128)S(1)} %copy.13) | data formatting | bytes 8192 | tf_op jit(solution)/shard_map/reshape | solution.py:350
  3.8 62.4 %transfer.1 = bf16[81,2048]{1,0:T(8,128)(2,1)} custom-call(s32[256,8192]{1,0:T(8,128)} %code_ref.1, s32[64]{0:T(128)} %count_ref.1, bf16[2,32,3,8,128]{4,3,2,1,0:T(8,128)(2,1)} %bitcast.8, s32[1024,1]{1,0:T(8,128)} %reshape.21.list_ref, f32[4,256,8]{2,1,0:T(8,128)} %constant.7.clone.axes_ref, f32[64,128]{1,0:T(8,128)} %bitcast.9, f32[64,128]{1,0:T(8,128)} %bitcast.10, ...), custom_call_target="tpu_custom_call" | custom-call | tf_op jit(solution)/shard_map/transfer/pallas_call | solution.py:314
  66.2 1.7 %copy.20 = bf16[81,2048]{1,0:T(8,128)(2,1)} copy(bf16[81,2048]{1,0:T(8,128)(2,1)} %transfer.1) | data formatting | bytes 663552

commit v3 on v2

v3 whole, which is shorter than its diff:
```python
import math

import jax
import jax.numpy as jnp
import numpy as np
from jax import lax
from jax.experimental import pallas as pl
from jax.experimental.pallas import tpu as pltpu
from jax.sharding import PartitionSpec as P

NDIR = 1024
SHORD = 9
COEFFS = 81
SLOTS = 16
CLUSTERS = 64
BLK = 8
DIRS = 256
HALF = 128
VERTS = 8192
OWN = 2048
KG = 32
PARTS = 3
ROWS = KG * PARTS
SEND = 88
FULL = COEFFS - KG * (PARTS - 1)
NB = 512
NI = 256
F32 = jnp.float32
BF16 = jnp.bfloat16
MESH = pl.DeviceIdType.MESH
SCALE = 4.0 * math.pi / NDIR
GOLDEN = math.pi * (3.0 - math.sqrt(5.0))


def direction_tables():
    p = np.arange(NDIR, dtype=np.float32)
    z = (np.float32(1.0) - (np.float32(2.0) * p + np.float32(1.0)) / np.float32(NDIR)).astype(np.float32)
    r = np.sqrt(np.maximum(np.float32(1.0) - z * z, np.float32(0.0)))
    t = (p * np.float32(GOLDEN)).astype(np.float64)
    x = (r * np.cos(t).astype(np.float32)).astype(np.float64)
    y = (r * np.sin(t).astype(np.float32)).astype(np.float64)
    z = z.astype(np.float64)
    c, s = [np.ones_like(x)], [np.zeros_like(x)]
    for _ in range(1, SHORD):
        c.append(c[-1] * x - s[-1] * y)
        s.append(c[-2] * y + s[-1] * x)
    rows = [None] * COEFFS
    for m in range(SHORD):
        q = [None] * SHORD
        q[m] = np.full_like(z, float(np.prod(np.arange(1, 2 * m, 2, dtype=np.float64))))
        if m + 1 < SHORD:
            q[m + 1] = z * (2 * m + 1) * q[m]
        for l in range(m + 2, SHORD):
            q[l] = ((2 * l - 1) * z * q[l - 1] - (l + m - 1) * q[l - 2]) / (l - m)
        for l in range(m, SHORD):
            n = math.sqrt((2 * l + 1) / (4.0 * math.pi) * math.factorial(l - m) / math.factorial(l + m))
            at = l * l + l
            if m == 0:
                rows[at] = n * q[l]
            else:
                rows[at + m] = math.sqrt(2.0) * n * q[l] * c[m]
                rows[at - m] = math.sqrt(2.0) * n * q[l] * s[m]
    table = np.zeros((4, ROWS, DIRS), np.float32)
    table[:, :COEFFS] = np.stack(rows).reshape(COEFFS, 4, DIRS).transpose(1, 0, 2)
    axes = np.zeros((4, DIRS, 8), np.float32)
    for i, a in enumerate((x, y, z)):
        axes[:, :, i] = a.reshape(4, DIRS)
    return table, axes


def place(x, z, core):
    return core, lax.rem((z * 4 + x) * 5, KG)


def transfer_kernel(
    code_ref, count_ref, block_hbm, list_hbm, axes_hbm, azimuth_hbm, height_hbm, albedo_hbm, harm_hbm, out_ref,
    list_ref, axes_ref, azimuth_ref, height_ref, albedo_ref, harm_ref, codes, weight, slot, direct, total, own, normal, chosen, turn, blocks, slices, picked, table, matrix, parts, got,
    load_sem, code_sem, send_a, recv_a, send_b, recv_b, send_sem, recv_sem,
):
    me = lax.axis_index("cluster")
    row = lax.axis_index("dir")
    my_x, my_z, my_core = lax.div(me, 16), lax.rem(lax.div(me, 2), 8), lax.rem(me, 2)
    my_half, my_group = place(my_x, my_z, my_core)
    steps = VERTS // NB
    subs = OWN // NB

    def peer_of(i):
        j, r = lax.div(i, 8), lax.rem(i, 8)
        m = lax.div(r, 2)
        z = lax.rem(my_z + 4 + lax.div(j + 1, 2) * (1 - 2 * lax.rem(j, 2)), 8)
        x = lax.rem(my_x + 2 + lax.div(m + 1, 2) * (1 - 2 * lax.rem(m, 2)), 4)
        core = lax.rem(my_core + 1 + r, 2)
        return x, z, core

    def at(x, z, core):
        return {"cluster": x * 16 + z * 2 + core}

    def first_of(t):
        pair, half = lax.div(t, subs), lax.rem(t, 2)
        ahead = lax.rem(2 + pair, 4) + lax.div(pair, 2) * (1 - 2 * lax.rem(pair, 2))
        ahead = ahead + 2 * half * lax.rem(lax.div(pair + 1, 2), 2)
        inner = half * (subs // 2) + lax.rem(lax.div(t, 2), subs // 2)
        return pl.multiple_of(lax.rem(row + ahead, 4) * OWN + inner * NB, NB)

    def fetch(t):
        return pltpu.make_async_copy(code_ref.at[:, pl.ds(first_of(t), NB)], codes.at[t], code_sem.at[t])

    loads = [
        pltpu.make_async_copy(source, target, load_sem.at[i])
        for i, (source, target) in enumerate(
            (
                (block_hbm, blocks),
                (list_hbm, list_ref),
                (azimuth_hbm, azimuth_ref),
                (height_hbm, height_ref),
                (albedo_hbm, albedo_ref),
                (axes_hbm.at[row], axes_ref),
                (harm_hbm.at[row], harm_ref),
            )
        )
    ]
    barrier = pltpu.get_barrier_semaphore()

    def greet(i, carry):
        pl.semaphore_signal(barrier, inc=1, device_id=at(*peer_of(i)), device_id_type=MESH)
        return carry

    lax.fori_loop(0, CLUSTERS - 1, greet, 0)
    for i in (1, 3):
        pl.semaphore_signal(barrier, inc=1, device_id={"dir": lax.rem(row + i, 4)}, device_id_type=MESH)

    for load in loads:
        load.start()

    def start_fetch(t, carry):
        fetch(t).start()
        return carry

    lax.fori_loop(0, steps, start_fetch, 0)

    for load in loads:
        load.wait()
    my_lanes = pl.ds(pl.multiple_of(my_half * HALF, HALF), HALF)
    for unit in range(PARTS - 1):
        slices[me, unit] = blocks[unit * KG + my_group, :, my_lanes]

    @pl.when(my_group < FULL)
    def _():
        slices[me, PARTS - 1] = blocks[(PARTS - 1) * KG + my_group, :, my_lanes]

    lists = jnp.broadcast_to(list_ref[...].astype(F32).T[:, None, :], (CLUSTERS, SLOTS, SLOTS))
    here = lax.broadcasted_iota(jnp.int32, lists.shape, 1) == lax.broadcasted_iota(jnp.int32, lists.shape, 2)
    column = jnp.sum(jnp.where(here, lists, 0.0), axis=2, keepdims=True).reshape(CLUSTERS * SLOTS, 1)
    each = lax.broadcasted_iota(jnp.int32, (CLUSTERS * SLOTS, CLUSTERS * BLK), 1).astype(F32)
    chosen[...] = jnp.where(column == each, 1.0, 0.0).astype(BF16)
    to = lax.broadcasted_iota(jnp.int32, (SLOTS * KG, SLOTS * KG), 0)
    fro = lax.broadcasted_iota(jnp.int32, (SLOTS * KG, SLOTS * KG), 1)
    turn[...] = jnp.where((to % KG) * SLOTS + to // KG == fro, 1.0, 0.0).astype(BF16)
    table[:, FULL:, PARTS - 1] = jnp.zeros((2, KG - FULL, SLOTS, HALF), BF16)
    height = height_ref[...]
    planar = jnp.sqrt(jnp.maximum(1.0 - height * height, 0.0))
    normal[0] = planar * jnp.cos(azimuth_ref[...])
    normal[1] = planar * jnp.sin(azimuth_ref[...])
    pl.semaphore_wait(barrier, CLUSTERS + 1)

    def first(peer, unit):
        half, group = place(*peer)
        return pltpu.make_async_remote_copy(
            src_ref=blocks.at[unit * KG + group, :, pl.ds(pl.multiple_of(half * HALF, HALF), HALF)],
            dst_ref=slices.at[me, unit],
            send_sem=send_a.at[unit],
            recv_sem=recv_a.at[unit],
            device_id=at(*peer),
            device_id_type=MESH,
        )

    def start_first(i, carry):
        first(peer_of(i), 0).start()
        return carry

    def start_first_rest(i, carry):
        peer = peer_of(i)
        first(peer, 1).start()

        @pl.when(place(*peer)[1] < FULL)
        def _():
            first(peer, 2).start()

        return carry

    lax.fori_loop(0, CLUSTERS - 1, start_first, 0)
    lax.fori_loop(0, CLUSTERS - 1, start_first_rest, 0)

    count = count_ref[me]
    x, y, z = (axes_ref[:, i : i + 1] for i in range(3))

    def across(ref, at):
        return jnp.concatenate([ref[pl.ds(at + i, 1), :] for i in range(NI // HALF)], axis=1)

    def prepare(t, carry):
        fetch(t).wait()
        base = lax.div(first_of(t), HALF)
        for n in range(NB // NI):
            cols = slice(n * NI, (n + 1) * NI)
            at = base + n * (NI // HALF)
            code = codes[t, :, cols]
            facing = jnp.maximum(
                x * across(normal.at[0], at) + y * across(normal.at[1], at) + z * across(height_ref, at), 0.0
            )
            hit = code < count
            weight[t, :, cols] = facing.astype(BF16)
            slot[t, :, cols] = jnp.where(hit, code, SLOTS).astype(jnp.int16)
            lit = jnp.where(hit, 0.0, facing)
            high = lit.astype(BF16)
            low = (lit - high.astype(F32)).astype(BF16)
            both = jnp.dot(harm_ref[...], high, preferred_element_type=F32)
            rest = jnp.dot(harm_ref[:ROWS], low, preferred_element_type=F32)
            direct[t, :, cols] = SCALE * (both[:ROWS] + both[ROWS:] + rest)
        return carry

    def choose(unit):
        others = slices.at[pl.ds(0, CLUSTERS - 1), unit]
        pltpu.make_async_copy(others, others, recv_a.at[unit]).wait()
        held = slices[:, unit].reshape(CLUSTERS * BLK, HALF)
        rows = jnp.dot(chosen[...], held, preferred_element_type=F32).astype(BF16)
        picked[:, unit] = rows.reshape(CLUSTERS, SLOTS, HALF)

    def second(i, unit):
        peer = peer_of(i)
        return pltpu.make_async_remote_copy(
            src_ref=picked.at[at_index(peer), unit],
            dst_ref=table.at[my_half, my_group, unit],
            send_sem=send_b.at[unit],
            recv_sem=recv_b.at[unit],
            device_id=at(*peer),
            device_id_type=MESH,
        )

    def at_index(peer):
        return peer[0] * 16 + peer[1] * 2 + peer[2]

    def start_second(unit):
        def body(i, carry):
            second(i, unit).start()
            return carry

        return body

    lax.fori_loop(0, 6, prepare, 0)
    choose(0)
    lax.fori_loop(0, CLUSTERS - 1, start_second(0), 0)
    lax.fori_loop(6, 8, prepare, 0)
    choose(1)
    lax.fori_loop(0, CLUSTERS - 1, start_second(1), 0)

    @pl.when(my_group < FULL)
    def _():
        choose(2)
        lax.fori_loop(0, CLUSTERS - 1, start_second(2), 0)
        table[my_half, my_group, 2] = picked[me, 2]

    for unit in range(PARTS - 1):
        table[my_half, my_group, unit] = picked[me, unit]

    lax.fori_loop(8, steps, prepare, 0)

    for unit in range(PARTS - 1):
        others = slices.at[pl.ds(0, CLUSTERS - 1), unit]
        sent = picked.at[pl.ds(0, CLUSTERS - 1), unit]
        pltpu.make_async_copy(others, others, send_a.at[unit]).wait()
        pltpu.make_async_copy(sent, sent, send_b.at[unit]).wait()

    def spread_part(i):
        both = jnp.concatenate([table[h, :, i].reshape(KG * SLOTS, HALF) for h in range(2)], axis=1)
        turned = jnp.dot(turn[...], both, preferred_element_type=F32).astype(BF16)
        matrix[:, i * KG : (i + 1) * KG, :] = turned.reshape(SLOTS, KG, DIRS)

    for unit in range(PARTS - 1):
        sent = picked.at[pl.ds(0, CLUSTERS - 1), unit]
        pltpu.make_async_copy(sent, sent, recv_b.at[unit]).wait()
        spread_part(unit)

    @pl.when(my_group < FULL)
    def _():
        fewer = slices.at[pl.ds(0, 2 * FULL - 1), 2]
        pltpu.make_async_copy(fewer, fewer, send_a.at[2]).wait()
        tail = picked.at[pl.ds(0, CLUSTERS - 1), 2]
        pltpu.make_async_copy(tail, tail, send_b.at[2]).wait()
        less = picked.at[pl.ds(0, 2 * FULL - 1), 2]
        pltpu.make_async_copy(less, less, recv_b.at[2]).wait()

    @pl.when(my_group >= FULL)
    def _():
        fewer = slices.at[pl.ds(0, 2 * FULL), 2]
        pltpu.make_async_copy(fewer, fewer, send_a.at[2]).wait()
        less = picked.at[pl.ds(0, 2 * FULL), 2]
        pltpu.make_async_copy(less, less, recv_b.at[2]).wait()

    spread_part(2)

    def exchange(t):
        way = (1 - 2 * lax.rem(t, 2)) * (1 - 2 * lax.rem(lax.div(t, subs), 2))
        return pltpu.make_async_remote_copy(
            src_ref=parts.at[t],
            dst_ref=got.at[t],
            send_sem=send_sem.at[t],
            recv_sem=recv_sem.at[t],
            device_id={"dir": lax.rem(row + way + 4, 4)},
            device_id_type=MESH,
        )

    wide = NB // HALF

    def pack(t, sums):
        for r in range(COEFFS // 8):
            for c in range(wide):
                parts[t, r * wide + c] = sums[r * 8 : r * 8 + 8, c * HALF : (c + 1) * HALF].astype(BF16)
        end = [sums[COEFFS - 1 : COEFFS, c * HALF : (c + 1) * HALF] for c in range(wide)]
        parts[t, COEFFS // 8 * wide] = jnp.concatenate(end * (8 // wide), axis=0).astype(BF16)

    def unpack(t):
        tiles = [got[t, i].astype(F32) for i in range(COEFFS // 8 * wide + 1)]
        rows = [jnp.concatenate(tiles[r * wide : (r + 1) * wide], axis=1) for r in range(COEFFS // 8)]
        end = jnp.concatenate([tiles[-1][c : c + 1] for c in range(wide)], axis=1)
        return jnp.concatenate(rows + [jnp.broadcast_to(end, (8, NB))], axis=0)

    def step(t, carry):
        base = lax.div(first_of(t), HALF)
        for n in range(NB // NI):
            cols = slice(n * NI, (n + 1) * NI)
            held, code = weight[t, :, cols], slot[t, :, cols]
            bounce = None
            for s in range(SLOTS):
                spread = jnp.where(code == jnp.int16(s), held, jnp.zeros_like(held))
                term = jnp.dot(matrix[s], spread, preferred_element_type=F32)
                bounce = term if bounce is None else bounce + term
            gain = SCALE * across(albedo_ref, base + n * (NI // HALF))
            total[:, cols] = direct[t, :, cols] + gain * bounce

        @pl.when(t < 2 * subs)
        def _():
            pack(t, total[:SEND])
            exchange(t).start()

        @pl.when(lax.div(t, subs) == 2)
        def _():
            exchange(t - 2 * subs).wait_recv()
            pack(t, total[:SEND] + unpack(t - 2 * subs))
            exchange(t).start()

        @pl.when(t >= 3 * subs)
        def _():
            own[t - 3 * subs] = total[:SEND]

        return carry

    lax.fori_loop(0, steps, step, 0)
    for i in range(subs):
        exchange(subs + i).wait_recv()
        exchange(2 * subs + i).wait_recv()
        mine = own[i] + unpack(subs + i) + unpack(2 * subs + i)
        begin = ((i % 2) * (subs // 2) + i // 2) * NB
        out_ref[:, begin : begin + NB] = mine[:COEFFS].astype(BF16)
    for t in range(3 * subs):
        exchange(t).wait_send()


def per_device(
    ray_code, occluder_list, list_count, normal_azimuth, normal_height, albedo, occluder_exit_radiance
):
    harmonics, axes = direction_tables()
    high = harmonics.astype(BF16)
    harmonics = np.concatenate([high, (harmonics - high.astype(np.float32)).astype(BF16)], axis=1)
    hbm = pl.BlockSpec(memory_space=pltpu.HBM)
    tiles = COEFFS // 8 * (NB // HALF) + 1
    steps = VERTS // NB
    sends = 3 * (OWN // NB)
    by_lane = (VERTS // HALF, HALF)
    dma = pltpu.SemaphoreType.DMA
    return pl.pallas_call(
        transfer_kernel,
        out_shape=jax.ShapeDtypeStruct((COEFFS, OWN), BF16),
        in_specs=[hbm, pl.BlockSpec(memory_space=pltpu.SMEM)] + [hbm] * 7,
        out_specs=pl.BlockSpec(memory_space=pltpu.VMEM),
        scratch_shapes=[
            pltpu.VMEM((SLOTS, CLUSTERS), jnp.int32),
            pltpu.VMEM((DIRS, 8), F32),
            pltpu.VMEM(by_lane, F32),
            pltpu.VMEM(by_lane, F32),
            pltpu.VMEM(by_lane, F32),
            pltpu.VMEM((2 * ROWS, DIRS), BF16),
            pltpu.VMEM((steps, DIRS, NB), jnp.int32),
            pltpu.VMEM((steps, DIRS, NB), BF16),
            pltpu.VMEM((steps, DIRS, NB), jnp.int16),
            pltpu.VMEM((steps, ROWS, NB), F32),
            pltpu.VMEM((ROWS, NB), F32),
            pltpu.VMEM((OWN // NB, SEND, NB), F32),
            pltpu.VMEM((2,) + by_lane, F32),
            pltpu.VMEM((CLUSTERS * SLOTS, CLUSTERS * BLK), BF16),
            pltpu.VMEM((SLOTS * KG, SLOTS * KG), BF16),
            pltpu.VMEM((COEFFS, BLK, DIRS), BF16),
            pltpu.VMEM((CLUSTERS, PARTS, BLK, HALF), BF16),
            pltpu.VMEM((CLUSTERS, PARTS, SLOTS, HALF), BF16),
            pltpu.VMEM((2, KG, PARTS, SLOTS, HALF), BF16),
            pltpu.VMEM((SLOTS, ROWS, DIRS), BF16),
            pltpu.VMEM((sends, tiles, 8, HALF), BF16),
            pltpu.VMEM((sends, tiles, 8, HALF), BF16),
            dma((7,)),
            dma((steps,)),
        ]
        + [dma((PARTS,))] * 4
        + [dma((sends,)), dma((sends,))],
        compiler_params=pltpu.CompilerParams(
            collective_id=0, has_side_effects=True, vmem_limit_bytes=60 << 20
        ),
        name="transfer",
    )(
        ray_code,
        list_count,
        occluder_exit_radiance.transpose(1, 0, 2),
        occluder_list.T,
        jnp.asarray(axes),
        normal_azimuth.reshape(by_lane),
        normal_height.reshape(by_lane),
        albedo.reshape(by_lane),
        jnp.asarray(harmonics),
    )


def solution(mesh):
    return jax.shard_map(
        per_device,
        mesh=mesh,
        in_specs=(
            P("dir", "cluster"),
            P(),
            P(),
            P("cluster"),
            P("cluster"),
            P("cluster"),
            P("cluster", None, "dir"),
        ),
        out_specs=P(None, ("cluster", "dir")),
        check_vma=False,
    )
```

time: 68.2 us -> 57.1 us (0.84)
  Pallas kernels: 62.4 us -> 55.2 us
  local copies, waits for them, and re-layouts: 5.52 us -> 1.74 us
    pallas_call x1, Pallas kernels: 62.4 us -> 55.2 us  [per_device(): pl.pallas_call(transfer_kernel, out_shape=jax.ShapeDtypeStruct((COEFFS, O...]
    reshape x3 -> x0, local copies, waits for them, and re-layouts: 1.99 us -> none  [the longest x1 1.09 us: per_device(): occluder_list.reshape(CLUSTERS * SLOTS, 1)]
    pad x1 -> x0, local copies, waits for them, and re-layouts: 1 us -> none  [per_device(): jnp.pad(occluder_exit_radiance, ((0, 0), (0, ROWS - COEFFS), (0, 0)))]
    unnamed x2 -> x1, local copies, waits for them, and re-layouts: 2.52 us -> 1.74 us
where the time goes in v3:
time: 57.1 us; the launch traced here: 56.9 us
  Pallas kernels  55.2 us (97%)
  local copies, waits for them, and re-layouts  1.74 us (3%)
    pallas_call x1, Pallas kernels, per_device(): pl.pallas_call(transfer_kernel, out_shape=jax.ShapeDtypeStruct((COEFFS, O...  55.2 us
    unnamed x1, local copies, waits for them, and re-layouts  1.74 us

profile of v3, /device:TPU:1, one launch (start us, length us, event | category | flops | bytes accessed | tf_op | source)
XLA Modules:
  0.0 56.9 jit_solution(4583743430541968128)
XLA Ops:
  0.0 55.2 %transfer.1 = bf16[81,2048]{1,0:T(8,128)(2,1)} custom-call(s32[256,8192]{1,0:T(8,128)} %code_ref.1, s32[64]{0:T(128)} %count_ref.1, bf16[81,8,256]{2,1,0:T(8,128)(2,1)} %bitcast.5, s32[16,64]{1,0:T(8,128)} %bitcast.9, f32[4,256,8]{2,1,0:T(8,128)} %constant.4.clone.axes_hbm, f32[64,128]{1,0:T(8,128)} %bitcast.6, f32[64,128]{1,0:T(8,128)} %bitcast.7, ...), custom_call_target="tpu_custom_call" | custom-call | tf_op jit(solution)/shard_map/transfer/pallas_call | solution.py:380
  55.2 1.7 %copy.11 = bf16[81,2048]{1,0:T(8,128)(2,1)} copy(bf16[81,2048]{1,0:T(8,128)(2,1)} %transfer.1) | data formatting | bytes 663552

commit v4 on v3

--- a/solution.py
+++ b/solution.py
@@ -73,8 +73,8 @@
 
 
 def transfer_kernel(
-    code_ref, count_ref, block_hbm, list_hbm, axes_hbm, azimuth_hbm, height_hbm, albedo_hbm, harm_hbm, out_ref,
-    list_ref, axes_ref, azimuth_ref, height_ref, albedo_ref, harm_ref, codes, weight, slot, direct, total, own, normal, chosen, turn, blocks, slices, picked, table, matrix, parts, got,
+    code_ref, count_hbm, block_hbm, list_hbm, axes_hbm, azimuth_hbm, height_hbm, albedo_hbm, harm_hbm, out_ref,
+    count_ref, list_ref, axes_ref, azimuth_ref, height_ref, albedo_ref, harm_ref, codes, weight, slot, direct, total, own, normal, chosen, turn, blocks, slices, picked, table, matrix, parts, got,
     load_sem, code_sem, send_a, recv_a, send_b, recv_b, send_sem, recv_sem,
 ):
     me = lax.axis_index("cluster")
@@ -84,13 +84,25 @@
     steps = VERTS // NB
     subs = OWN // NB
 
-    def peer_of(i):
-        j, r = lax.div(i, 8), lax.rem(i, 8)
-        m = lax.div(r, 2)
-        z = lax.rem(my_z + 4 + lax.div(j + 1, 2) * (1 - 2 * lax.rem(j, 2)), 8)
-        x = lax.rem(my_x + 2 + lax.div(m + 1, 2) * (1 - 2 * lax.rem(m, 2)), 4)
-        core = lax.rem(my_core + 1 + r, 2)
-        return x, z, core
+    columns = [lax.rem(my_x + i, 4) for i in range(4)]
+    cores = [my_core, 1 - my_core]
+
+    def each_peer(act):
+        def visit(j, carry):
+            z = lax.rem(my_z + 4 + lax.div(j + 1, 2) * (1 - 2 * lax.rem(j, 2)), 8)
+            for dx in (2, 1, 3, 0):
+                for flip in (1, 0):
+                    if dx or flip:
+                        act((columns[dx], z, cores[flip]))
+                    else:
+
+                        @pl.when(j < 7)
+                        def _():
+                            act((columns[0], z, cores[0]))
+
+            return carry
+
+        lax.fori_loop(0, 8, visit, 0)
 
     def at(x, z, core):
         return {"cluster": x * 16 + z * 2 + core}
@@ -110,6 +122,7 @@
         for i, (source, target) in enumerate(
             (
                 (block_hbm, blocks),
+                (count_hbm, count_ref),
                 (list_hbm, list_ref),
                 (azimuth_hbm, azimuth_ref),
                 (height_hbm, height_ref),
@@ -121,11 +134,10 @@
     ]
     barrier = pltpu.get_barrier_semaphore()
 
-    def greet(i, carry):
-        pl.semaphore_signal(barrier, inc=1, device_id=at(*peer_of(i)), device_id_type=MESH)
-        return carry
-
-    lax.fori_loop(0, CLUSTERS - 1, greet, 0)
+    def greet(peer):
+        pl.semaphore_signal(barrier, inc=1, device_id=at(*peer), device_id_type=MESH)
+
+    each_peer(greet)
     for i in (1, 3):
         pl.semaphore_signal(barrier, inc=1, device_id={"dir": lax.rem(row + i, 4)}, device_id_type=MESH)
 
@@ -174,22 +186,18 @@
             device_id_type=MESH,
         )
 
-    def start_first(i, carry):
-        first(peer_of(i), 0).start()
-        return carry
-
-    def start_first_rest(i, carry):
-        peer = peer_of(i)
+    def start_first(peer):
+        first(peer, 0).start()
+
+    def start_first_rest(peer):
         first(peer, 1).start()
 
         @pl.when(place(*peer)[1] < FULL)
         def _():
             first(peer, 2).start()
 
-        return carry
-
-    lax.fori_loop(0, CLUSTERS - 1, start_first, 0)
-    lax.fori_loop(0, CLUSTERS - 1, start_first_rest, 0)
+    each_peer(start_first)
+    each_peer(start_first_rest)
 
     count = count_ref[me]
     x, y, z = (axes_ref[:, i : i + 1] for i in range(3))
@@ -225,38 +233,30 @@
         rows = jnp.dot(chosen[...], held, preferred_element_type=F32).astype(BF16)
         picked[:, unit] = rows.reshape(CLUSTERS, SLOTS, HALF)
 
-    def second(i, unit):
-        peer = peer_of(i)
-        return pltpu.make_async_remote_copy(
-            src_ref=picked.at[at_index(peer), unit],
-            dst_ref=table.at[my_half, my_group, unit],
-            send_sem=send_b.at[unit],
-            recv_sem=recv_b.at[unit],
-            device_id=at(*peer),
-            device_id_type=MESH,
-        )
-
-    def at_index(peer):
-        return peer[0] * 16 + peer[1] * 2 + peer[2]
-
-    def start_second(unit):
-        def body(i, carry):
-            second(i, unit).start()
-            return carry
-
-        return body
-
-    lax.fori_loop(0, 6, prepare, 0)
+    def second(unit):
+        def start(peer):
+            pltpu.make_async_remote_copy(
+                src_ref=picked.at[at(*peer)["cluster"], unit],
+                dst_ref=table.at[my_half, my_group, unit],
+                send_sem=send_b.at[unit],
+                recv_sem=recv_b.at[unit],
+                device_id=at(*peer),
+                device_id_type=MESH,
+            ).start()
+
+        each_peer(start)
+
+    lax.fori_loop(0, 4, prepare, 0)
     choose(0)
-    lax.fori_loop(0, CLUSTERS - 1, start_second(0), 0)
-    lax.fori_loop(6, 8, prepare, 0)
+    second(0)
+    lax.fori_loop(4, 8, prepare, 0)
     choose(1)
-    lax.fori_loop(0, CLUSTERS - 1, start_second(1), 0)
+    second(1)
 
     @pl.when(my_group < FULL)
     def _():
         choose(2)
-        lax.fori_loop(0, CLUSTERS - 1, start_second(2), 0)
+        second(2)
         table[my_half, my_group, 2] = picked[me, 2]
 
     for unit in range(PARTS - 1):
@@ -377,12 +377,27 @@
     sends = 3 * (OWN // NB)
     by_lane = (VERTS // HALF, HALF)
     dma = pltpu.SemaphoreType.DMA
+    held = [
+        pltpu.with_memory_space_constraint(a, pltpu.HBM)
+        for a in (
+            ray_code,
+            list_count,
+            occluder_exit_radiance.transpose(1, 0, 2),
+            occluder_list.T,
+            jnp.asarray(axes),
+            normal_azimuth.reshape(by_lane),
+            normal_height.reshape(by_lane),
+            albedo.reshape(by_lane),
+            jnp.asarray(harmonics),
+        )
+    ]
     return pl.pallas_call(
         transfer_kernel,
         out_shape=jax.ShapeDtypeStruct((COEFFS, OWN), BF16),
-        in_specs=[hbm, pl.BlockSpec(memory_space=pltpu.SMEM)] + [hbm] * 7,
+        in_specs=[hbm] * 9,
         out_specs=pl.BlockSpec(memory_space=pltpu.VMEM),
         scratch_shapes=[
+            pltpu.SMEM((CLUSTERS,), jnp.int32),
             pltpu.VMEM((SLOTS, CLUSTERS), jnp.int32),
             pltpu.VMEM((DIRS, 8), F32),
             pltpu.VMEM(by_lane, F32),
@@ -405,26 +420,16 @@
             pltpu.VMEM((SLOTS, ROWS, DIRS), BF16),
             pltpu.VMEM((sends, tiles, 8, HALF), BF16),
             pltpu.VMEM((sends, tiles, 8, HALF), BF16),
-            dma((7,)),
+            dma((8,)),
             dma((steps,)),
         ]
         + [dma((PARTS,))] * 4
         + [dma((sends,)), dma((sends,))],
         compiler_params=pltpu.CompilerParams(
-            collective_id=0, has_side_effects=True, vmem_limit_bytes=60 << 20
+            collective_id=0, has_side_effects=True, vmem_limit_bytes=40 << 20
         ),
         name="transfer",
-    )(
-        ray_code,
-        list_count,
-        occluder_exit_radiance.transpose(1, 0, 2),
-        occluder_list.T,
-        jnp.asarray(axes),
-        normal_azimuth.reshape(by_lane),
-        normal_height.reshape(by_lane),
-        albedo.reshape(by_lane),
-        jnp.asarray(harmonics),
-    )
+    )(*held)
 
 
 def solution(mesh):

time: 57.1 us -> 53.9 us (0.944)
  Pallas kernels: 55.2 us -> 53.1 us
  local copies, waits for them, and re-layouts: 1.74 us -> 0.74 us
    pallas_call x1, Pallas kernels: 55.2 us -> 53.1 us  [per_device(): pl.pallas_call(transfer_kernel, out_shape=jax.ShapeDtypeStruct((COEFFS, O...]
    unnamed x1, local copies, waits for them, and re-layouts: 1.74 us -> 0.74 us
where the time goes in v4:
time: 53.9 us; the launch traced here: 53.8 us
  Pallas kernels  53.1 us (99%)
  local copies, waits for them, and re-layouts  0.74 us (1%)
    pallas_call x1, Pallas kernels, per_device(): pl.pallas_call(transfer_kernel, out_shape=jax.ShapeDtypeStruct((COEFFS, O...  53.1 us

profile of v4, /device:TPU:1, one launch (start us, length us, event | category | flops | bytes accessed | tf_op | source)
XLA Modules:
  0.0 53.8 jit_solution(8860051032553989999)
XLA Ops:
  0.0 53.1 %transfer.1 = bf16[81,2048]{1,0:T(8,128)(2,1)S(1)} custom-call(s32[256,8192]{1,0:T(8,128)} %code_ref.1, s32[64]{0:T(128)} %count_hbm.1, bf16[81,8,256]{2,1,0:T(8,128)(2,1)} %bitcast.5, s32[16,64]{1,0:T(8,128)} %bitcast.9, f32[4,256,8]{2,1,0:T(8,128)} %constant.4.clone.axes_hbm, f32[64,128]{1,0:T(8,128)} %bitcast.6, f32[64,128]{1,0:T(8,128)} %bitcast.7, ...), custom_call_target="tpu_custom_call" | custom-call | tf_op jit(solution)/shard_map/transfer/pallas_call | solution.py:394
  53.1 0.7 %copy.11 = bf16[81,2048]{1,0:T(8,128)(2,1)} copy(bf16[81,2048]{1,0:T(8,128)(2,1)S(1)} %transfer.1) | data formatting | bytes 663552

commit v5 on v4

--- a/solution.py
+++ b/solution.py
@@ -264,12 +264,6 @@
 
     lax.fori_loop(8, steps, prepare, 0)
 
-    for unit in range(PARTS - 1):
-        others = slices.at[pl.ds(0, CLUSTERS - 1), unit]
-        sent = picked.at[pl.ds(0, CLUSTERS - 1), unit]
-        pltpu.make_async_copy(others, others, send_a.at[unit]).wait()
-        pltpu.make_async_copy(sent, sent, send_b.at[unit]).wait()
-
     def spread_part(i):
         both = jnp.concatenate([table[h, :, i].reshape(KG * SLOTS, HALF) for h in range(2)], axis=1)
         turned = jnp.dot(turn[...], both, preferred_element_type=F32).astype(BF16)
@@ -282,17 +276,11 @@
 
     @pl.when(my_group < FULL)
     def _():
-        fewer = slices.at[pl.ds(0, 2 * FULL - 1), 2]
-        pltpu.make_async_copy(fewer, fewer, send_a.at[2]).wait()
-        tail = picked.at[pl.ds(0, CLUSTERS - 1), 2]
-        pltpu.make_async_copy(tail, tail, send_b.at[2]).wait()
         less = picked.at[pl.ds(0, 2 * FULL - 1), 2]
         pltpu.make_async_copy(less, less, recv_b.at[2]).wait()
 
     @pl.when(my_group >= FULL)
     def _():
-        fewer = slices.at[pl.ds(0, 2 * FULL), 2]
-        pltpu.make_async_copy(fewer, fewer, send_a.at[2]).wait()
         less = picked.at[pl.ds(0, 2 * FULL), 2]
         pltpu.make_async_copy(less, less, recv_b.at[2]).wait()
 
@@ -363,6 +351,23 @@
         out_ref[:, begin : begin + NB] = mine[:COEFFS].astype(BF16)
     for t in range(3 * subs):
         exchange(t).wait_send()
+    for unit in range(PARTS - 1):
+        others = slices.at[pl.ds(0, CLUSTERS - 1), unit]
+        sent = picked.at[pl.ds(0, CLUSTERS - 1), unit]
+        pltpu.make_async_copy(others, others, send_a.at[unit]).wait()
+        pltpu.make_async_copy(sent, sent, send_b.at[unit]).wait()
+
+    @pl.when(my_group < FULL)
+    def _():
+        fewer = slices.at[pl.ds(0, 2 * FULL - 1), 2]
+        pltpu.make_async_copy(fewer, fewer, send_a.at[2]).wait()
+        tail = picked.at[pl.ds(0, CLUSTERS - 1), 2]
+        pltpu.make_async_copy(tail, tail, send_b.at[2]).wait()
+
+    @pl.when(my_group >= FULL)
+    def _():
+        fewer = slices.at[pl.ds(0, 2 * FULL), 2]
+        pltpu.make_async_copy(fewer, fewer, send_a.at[2]).wait()
 
 
 def per_device(

time: 53.9 us -> 53.9 us (level)
  no operation moved by 1% of the time
where the time goes in v5:
time: 53.9 us; the launch traced here: 53.8 us
  Pallas kernels  53.1 us (99%)
  local copies, waits for them, and re-layouts  0.74 us (1%)
    pallas_call x1, Pallas kernels, per_device(): pl.pallas_call(transfer_kernel, out_shape=jax.ShapeDtypeStruct((COEFFS, O...  53.1 us

profile of v5, /device:TPU:1, one launch (start us, length us, event | category | flops | bytes accessed | tf_op | source)
XLA Modules:
  0.0 53.8 jit_solution(18192379879105292928)
XLA Ops:
  0.0 53.1 %transfer.1 = bf16[81,2048]{1,0:T(8,128)(2,1)S(1)} custom-call(s32[256,8192]{1,0:T(8,128)} %code_ref.1, s32[64]{0:T(128)} %count_hbm.1, bf16[81,8,256]{2,1,0:T(8,128)(2,1)} %bitcast.5, s32[16,64]{1,0:T(8,128)} %bitcast.9, f32[4,256,8]{2,1,0:T(8,128)} %constant.4.clone.axes_hbm, f32[64,128]{1,0:T(8,128)} %bitcast.6, f32[64,128]{1,0:T(8,128)} %bitcast.7, ...), custom_call_target="tpu_custom_call" | custom-call | tf_op jit(solution)/shard_map/transfer/pallas_call | solution.py:399
  53.1 0.7 %copy.11 = bf16[81,2048]{1,0:T(8,128)(2,1)} copy(bf16[81,2048]{1,0:T(8,128)(2,1)S(1)} %transfer.1) | data formatting | bytes 663552
